TPU v7x, 32 devices: a whole 2x2x4 slice. The times are simulated.
32 devices in a mesh: tm: 8 (over z, x), space: 4 (over y, core).
Axes of the slice: x: 2, y: 2, z: 4, core: 2. Of those that a mesh axis runs over, the one named last changes fastest.
Arguments:
- checkpoint: float32 [8, 4, 64, 1024], P('tm', None, 'space'), may hold values from -6 to 6
- advect: float32 [8, 2, 64, 1024], P('tm', None, 'space'), may hold values from -0.2 to 0.2
- diffuse: float32 [8, 64, 1024], P('tm', 'space'), may hold values from 0.1 to 0.2
- obs_rows: int32 [8, 8, 8], P('tm', None, 'space'), may hold values from 0 to 1
- obs_values: float32 [8, 8, 8, 4, 8, 1024], P('tm', None, 'space'), may hold values from -6 to 6
- obs_weight: float32 [8], P('tm'), may hold values from 0.5 to 13.5
- error_inverse: float32 [8, 4], P('tm'), may hold values from 0.3 to 3
- rates: float32 [8, 4], replicated, may hold values from 0.07924466 to 1, as said below
Outputs:
- direction: float32 [8, 4, 64, 1024], P('tm', None, 'space')
- grad_rms: float32 [], replicated
Inputs may be any that keep to these rules, and one draw needn't show every extreme that they name: `obs_rows`: entry i of the last dimension counts blocks of 8 rows within the rows of space block i // 2; repeats may occur. `rates`: every entry is below 1.
All inputs are finite; a program needn't handle non-finite values.
Results may differ from a plain program's by a relative error of at most 0.0003.
Values sent between devices are 32-bit elements; how exact they have to be, the bound alone decides.
A program may use at most 64 MiB of HBM per device.

v0:
```python
import jax
import jax.numpy as jnp
from jax import lax
from jax.sharding import PartitionSpec as P

STEPS = 8
BLOCK = 8


def padded_2(block, sides, width):
    for axis, dim in sides:
        count = lax.axis_size(axis)
        forward = [(i, i + 1) for i in range(count - 1)]
        backward = [(target, source) for source, target in forward]
        low = lax.ppermute(
            lax.slice_in_dim(block, block.shape[dim] - width, None, axis=dim), axis, forward
        )
        high = lax.ppermute(lax.slice_in_dim(block, 0, width, axis=dim), axis, backward)
        block = jnp.concatenate([low, block, high], axis=dim)
    return block


def passed_along(value, axis, steps):
    count = lax.axis_size(axis)
    leading, last = (max(0, -steps), min(count, count - steps))
    return lax.ppermute(value, axis, [(source, source + steps) for source in range(leading, last)])


def stencil_of(advect_one, diffuse_one):
    centre = 1.0 - 4.0 * diffuse_one
    to_east = diffuse_one - 0.5 * advect_one[0]
    to_west = diffuse_one + 0.5 * advect_one[0]
    to_north = diffuse_one - 0.5 * advect_one[1]
    to_south = diffuse_one + 0.5 * advect_one[1]
    return (centre, to_east, to_west, to_north, to_south)


def advance(field_now, stencil):
    centre, to_east, to_west, to_north, to_south = stencil
    padded = padded_2(field_now, (("space", 1),), 1)
    return (
        centre * field_now
        + to_east * jnp.roll(field_now, -1, axis=2)
        + to_west * jnp.roll(field_now, 1, axis=2)
        + to_north * padded[:, 2:]
        + to_south * padded[:, :-2]
    )


def retreat(costate, stencil, north_pad, south_pad):
    padded = padded_2(costate, (("space", 1),), 1)
    centre, to_east, to_west = (stencil[0], stencil[1], stencil[2])
    return (
        centre * costate
        + jnp.roll(to_east * costate, 1, axis=2)
        + jnp.roll(to_west * costate, -1, axis=2)
        + (north_pad * padded)[:, :-2]
        + (south_pad * padded)[:, 2:]
    )


def select_rows(field_now, picker):
    blocks = field_now.reshape(field_now.shape[0], picker.shape[1], BLOCK, field_now.shape[2])
    return jnp.einsum("kb,cbrx->kcrx", picker, blocks, precision=lax.Precision.HIGHEST)


def spread_rows(misfit, picker, field_shape):
    placed = jnp.einsum("kb,kcrx->cbrx", picker, misfit, precision=lax.Precision.HIGHEST)
    return placed.reshape(field_shape)


def weigh_own(field_now, initial, inverse_row):
    prior_end = passed_along(field_now, "tm", 1)
    return inverse_row[:, None, None] * (initial - prior_end)


def adjoint_sweep(misfits, pickers, weight, later_term, stencil, north_pad, south_pad, field_shape):
    costate = spread_rows(weight * misfits[STEPS - 1], pickers[STEPS - 1], field_shape) - later_term
    for moment in range(STEPS, 0, -1):
        costate = retreat(costate, stencil, north_pad, south_pad)
        if moment >= 2:
            costate = costate + spread_rows(
                weight * misfits[moment - 2], pickers[moment - 2], field_shape
            )
    return costate


def combine(earlier, latter):
    return (earlier[0] * latter[0], latter[0] * earlier[1] + latter[1])


def on_device(checkpoint, advect, diffuse, obs_rows, obs_values, obs_weight, error_inverse, rates):
    initial = checkpoint[0]
    field_shape = initial.shape
    stencil = stencil_of(advect[0], diffuse[0])
    rim_coefs = padded_2(jnp.stack([advect[0, 1], diffuse[0]]), (("space", 1),), 1)
    north_pad = rim_coefs[1] - 0.5 * rim_coefs[0]
    south_pad = rim_coefs[1] + 0.5 * rim_coefs[0]
    block_count = field_shape[1] // BLOCK
    block_ids = jnp.arange(block_count, dtype=jnp.int32)
    pickers = [
        (obs_rows[0, moment][:, None] == block_ids[None, :]).astype(jnp.float32)
        for moment in range(STEPS)
    ]
    field_now = initial
    misfits = []
    for moment in range(STEPS):
        field_now = advance(field_now, stencil)
        misfits.append(select_rows(field_now, pickers[moment]) - obs_values[0, moment])
    weight = obs_weight[0]
    weighted = weigh_own(field_now, initial, error_inverse[0])
    later_term = passed_along(weighted, "tm", -1)
    costate = adjoint_sweep(
        misfits, pickers, weight, later_term, stencil, north_pad, south_pad, field_shape
    )
    gradient = costate + weighted
    square_sum = lax.psum(jnp.sum(gradient * gradient), ("tm", "space"))
    entries = lax.axis_size("tm") * lax.axis_size("space") * gradient.size
    rms_value = jnp.sqrt(square_sum / entries + 1e-06)
    position = lax.axis_index("tm")
    windows = lax.axis_size("tm")
    innovation = jnp.sqrt(1.0 - rates * rates)
    next_rates = jnp.concatenate([rates[1:], jnp.zeros((1, rates.shape[1]), jnp.float32)], axis=0)
    column_count = gradient.size // windows
    flat_grad = gradient.reshape(1, gradient.size)
    columns = lax.all_to_all(flat_grad, "tm", split_axis=1, concat_axis=0, tiled=True)
    places = position * column_count + jnp.arange(column_count, dtype=jnp.int32)
    member = places // (field_shape[1] * field_shape[2])
    onehot = (member[None, :] == jnp.arange(field_shape[0], dtype=jnp.int32)[:, None]).astype(
        jnp.float32
    )
    rate_cols = jnp.dot(rates, onehot, precision=lax.Precision.HIGHEST)
    inno_cols = jnp.dot(innovation, onehot, precision=lax.Precision.HIGHEST)
    next_cols = jnp.dot(next_rates, onehot, precision=lax.Precision.HIGHEST)
    forward_cols = lax.associative_scan(combine, (rate_cols, inno_cols * columns), axis=0)[1]
    backward_cols = lax.associative_scan(
        combine, (next_cols, inno_cols * forward_cols), reverse=True, axis=0
    )[1]
    flat_back = lax.all_to_all(backward_cols, "tm", split_axis=0, concat_axis=1, tiled=True)
    smoothed = flat_back.reshape(field_shape)
    direction = (smoothed / rms_value)[None]
    return (direction, rms_value)


def solution(mesh):
    placed = (
        P("tm", None, "space", None),
        P("tm", None, "space", None),
        P("tm", "space", None),
        P("tm", None, "space"),
        P("tm", None, "space", None, None, None),
        P("tm"),
        P("tm", None),
        P(),
    )
    return jax.shard_map(
        on_device,
        mesh=mesh,
        in_specs=placed,
        out_specs=(P("tm", None, "space", None), P()),
        check_vma=False,
    )
```

profile of v0, /device:TPU:0, one launch (start us, length us, event | category | flops | bytes accessed | tf_op | source)
XLA Modules:
  0.0 239.0 jit_solution(10749359197541015536)
XLA Ops:
  1.6 2.4 %collective-permute-start.1 = (f32[4,1,1024]{2,1,0:T(1,128)S(1)}, f32[4,1,1024]{2,1,0:T(1,128)S(1)}, u32[]{:S(2)}, u32[]{:S(2)}) collective-permute-start(f32[4,1,1024]{2,1,0:T(1,128)S(1)} %get-tuple-element.99), channel_id=1, source_target_pairs={{0,1},{1,2},{2,3},{4,5},{5,6},{6,7},{8,9},{9,10},{10,11},{12,13},{... | collective-permute-start | bytes 49160 | tf_op jit(solution)/shard_map/ppermute | solution.py:15
  4.0 1.3 collective-permute-start
  7.0 1.3 collective-permute-start.19
  8.3 5.8 %collective-permute-start.18 = (f32[2,1,1024]{2,1,0:T(1,128)S(1)}, f32[2,1,1024]{2,1,0:T(1,128)S(1)}, u32[]{:S(2)}, u32[]{:S(2)}) collective-permute-start(f32[2,1,1024]{2,1,0:T(1,128)S(1)} %get-tuple-element.114), channel_id=1, source_target_pairs={{0,1},{1,2},{2,3},{4,5},{5,6},{6,7},{8,9},{9,10},{10,11},{12,13},{... | collective-permute-start | bytes 24584 | tf_op jit(solution)/shard_map/ppermute | solution.py:15
  17.1 1.7 fusion.161
  20.3 3.6 %collective-permute-start.3 = (f32[4,1,1024]{2,1,0:T(1,128)S(1)}, f32[4,1,1024]{2,1,0:T(1,128)S(1)}, u32[]{:S(2)}, u32[]{:S(2)}) collective-permute-start(f32[4,1,1024]{2,1,0:T(1,128)S(1)} %get-tuple-element.93), channel_id=1, source_target_pairs={{0,1},{1,2},{2,3},{4,5},{5,6},{6,7},{8,9},{9,10},{10,11},{12,13},{... | collective-permute-start | bytes 49160 | tf_op jit(solution)/shard_map/ppermute | solution.py:15
  24.0 1.3 collective-permute-start.2
  27.4 4.4 %collective-permute-start.5 = (f32[4,1,1024]{2,1,0:T(1,128)S(1)}, f32[4,1,1024]{2,1,0:T(1,128)S(1)}, u32[]{:S(2)}, u32[]{:S(2)}) collective-permute-start(f32[4,1,1024]{2,1,0:T(1,128)S(1)} %get-tuple-element.87), channel_id=1, source_target_pairs={{0,1},{1,2},{2,3},{4,5},{5,6},{6,7},{8,9},{9,10},{10,11},{12,13},{... | collective-permute-start | bytes 49160 | tf_op jit(solution)/shard_map/ppermute | solution.py:15
  31.8 1.3 collective-permute-start.4
  35.2 4.2 %collective-permute-start.7 = (f32[4,1,1024]{2,1,0:T(1,128)S(1)}, f32[4,1,1024]{2,1,0:T(1,128)S(1)}, u32[]{:S(2)}, u32[]{:S(2)}) collective-permute-start(f32[4,1,1024]{2,1,0:T(1,128)S(1)} %get-tuple-element.81), channel_id=1, source_target_pairs={{0,1},{1,2},{2,3},{4,5},{5,6},{6,7},{8,9},{9,10},{10,11},{12,13},{... | collective-permute-start | bytes 49160 | tf_op jit(solution)/shard_map/ppermute | solution.py:15
  39.4 1.3 collective-permute-start.6
  42.8 4.2 %collective-permute-start.9 = (f32[4,1,1024]{2,1,0:T(1,128)S(1)}, f32[4,1,1024]{2,1,0:T(1,128)S(1)}, u32[]{:S(2)}, u32[]{:S(2)}) collective-permute-start(f32[4,1,1024]{2,1,0:T(1,128)S(1)} %get-tuple-element.75), channel_id=1, source_target_pairs={{0,1},{1,2},{2,3},{4,5},{5,6},{6,7},{8,9},{9,10},{10,11},{12,13},{... | collective-permute-start | bytes 49160 | tf_op jit(solution)/shard_map/ppermute | solution.py:15
  46.9 1.3 collective-permute-start.8
  50.4 4.2 %collective-permute-start.11 = (f32[4,1,1024]{2,1,0:T(1,128)S(1)}, f32[4,1,1024]{2,1,0:T(1,128)S(1)}, u32[]{:S(2)}, u32[]{:S(2)}) collective-permute-start(f32[4,1,1024]{2,1,0:T(1,128)S(1)} %get-tuple-element.69), channel_id=1, source_target_pairs={{0,1},{1,2},{2,3},{4,5},{5,6},{6,7},{8,9},{9,10},{10,11},{12,13},{... | collective-permute-start | bytes 49160 | tf_op jit(solution)/shard_map/ppermute | solution.py:15
  54.5 1.3 collective-permute-start.10
  57.9 4.2 %collective-permute-start.13 = (f32[4,1,1024]{2,1,0:T(1,128)S(1)}, f32[4,1,1024]{2,1,0:T(1,128)S(1)}, u32[]{:S(2)}, u32[]{:S(2)}) collective-permute-start(f32[4,1,1024]{2,1,0:T(1,128)S(1)} %get-tuple-element.63), channel_id=1, source_target_pairs={{0,1},{1,2},{2,3},{4,5},{5,6},{6,7},{8,9},{9,10},{10,11},{12,13},{... | collective-permute-start | bytes 49160 | tf_op jit(solution)/shard_map/ppermute | solution.py:15
  62.1 1.5 collective-permute-start.12
  65.6 4.1 %collective-permute-start.15 = (f32[4,1,1024]{2,1,0:T(1,128)S(1)}, f32[4,1,1024]{2,1,0:T(1,128)S(1)}, u32[]{:S(2)}, u32[]{:S(2)}) collective-permute-start(f32[4,1,1024]{2,1,0:T(1,128)S(1)} %get-tuple-element.57), channel_id=1, source_target_pairs={{0,1},{1,2},{2,3},{4,5},{5,6},{6,7},{8,9},{9,10},{10,11},{12,13},{... | collective-permute-start | bytes 49160 | tf_op jit(solution)/shard_map/ppermute | solution.py:15
  69.7 1.3 collective-permute-start.14
  71.1 1.7 collective-permute-done.14
  73.0 3.4 %collective-permute-start.16 = (f32[4,16,1024]{2,1,0:T(8,128)S(1)}, f32[4,16,1024]{2,1,0:T(8,128)S(1)}, u32[]{:S(2)}, u32[]{:S(2)}) collective-permute-start(f32[4,16,1024]{2,1,0:T(8,128)S(1)} %fusion.33), channel_id=1, source_target_pairs={{0,4},{4,8},{8,12},{12,16},{16,20},{20,24},{24,28},{1,5},{5,9},{9,... | collective-permute-start | bytes 786440 | tf_op jit(solution)/shard_map/ppermute | solution.py:26
  78.0 3.6 %collective-permute-done.16 = f32[4,16,1024]{2,1,0:T(8,128)S(1)} collective-permute-done((f32[4,16,1024]{2,1,0:T(8,128)S(1)}, f32[4,16,1024]{2,1,0:T(8,128)S(1)}, u32[]{:S(2)}, u32[]{:S(2)}) %collective-permute-start.16) | collective-permute-done | bytes 262176 | tf_op jit(solution)/shard_map/ppermute | solution.py:26
  81.7 1.3 collective-permute-start.17
  84.6 8.1 %collective-permute-done.17 = f32[4,16,1024]{2,1,0:T(8,128)S(1)} collective-permute-done((f32[4,16,1024]{2,1,0:T(8,128)S(1)}, f32[4,16,1024]{2,1,0:T(8,128)S(1)}, u32[]{:S(2)}, u32[]{:S(2)}) %collective-permute-start.17) | collective-permute-done | bytes 262176 | tf_op jit(solution)/shard_map/ppermute | solution.py:26
  92.8 1.3 collective-permute-start.21
  94.1 3.0 %collective-permute-start.20 = (f32[4,1,1024]{2,1,0:T(1,128)S(1)}, f32[4,1,1024]{2,1,0:T(1,128)S(1)}, u32[]{:S(2)}, u32[]{:S(2)}) collective-permute-start(f32[4,1,1024]{2,1,0:T(1,128)S(1)} %get-tuple-element.50), channel_id=1, source_target_pairs={{0,1},{1,2},{2,3},{4,5},{5,6},{6,7},{8,9},{9,10},{10,11},{12,13},{... | collective-permute-start | bytes 49160 | tf_op jit(solution)/shard_map/ppermute | solution.py:15
  98.3 1.3 collective-permute-start.23
  99.6 4.2 %collective-permute-start.22 = (f32[4,1,1024]{2,1,0:T(1,128)S(1)}, f32[4,1,1024]{2,1,0:T(1,128)S(1)}, u32[]{:S(2)}, u32[]{:S(2)}) collective-permute-start(f32[4,1,1024]{2,1,0:T(1,128)S(1)} %get-tuple-element.48), channel_id=1, source_target_pairs={{0,1},{1,2},{2,3},{4,5},{5,6},{6,7},{8,9},{9,10},{10,11},{12,13},{... | collective-permute-start | bytes 49160 | tf_op jit(solution)/shard_map/ppermute | solution.py:15
  105.0 1.3 collective-permute-start.25
  106.3 4.9 %collective-permute-start.24 = (f32[4,1,1024]{2,1,0:T(1,128)S(1)}, f32[4,1,1024]{2,1,0:T(1,128)S(1)}, u32[]{:S(2)}, u32[]{:S(2)}) collective-permute-start(f32[4,1,1024]{2,1,0:T(1,128)S(1)} %get-tuple-element.46), channel_id=1, source_target_pairs={{0,1},{1,2},{2,3},{4,5},{5,6},{6,7},{8,9},{9,10},{10,11},{12,13},{... | collective-permute-start | bytes 49160 | tf_op jit(solution)/shard_map/ppermute | solution.py:15
  112.3 1.3 collective-permute-start.27
  113.6 4.9 %collective-permute-start.26 = (f32[4,1,1024]{2,1,0:T(1,128)S(1)}, f32[4,1,1024]{2,1,0:T(1,128)S(1)}, u32[]{:S(2)}, u32[]{:S(2)}) collective-permute-start(f32[4,1,1024]{2,1,0:T(1,128)S(1)} %get-tuple-element.44), channel_id=1, source_target_pairs={{0,1},{1,2},{2,3},{4,5},{5,6},{6,7},{8,9},{9,10},{10,11},{12,13},{... | collective-permute-start | bytes 49160 | tf_op jit(solution)/shard_map/ppermute | solution.py:15
  119.6 1.3 collective-permute-start.29
  120.9 4.9 %collective-permute-start.28 = (f32[4,1,1024]{2,1,0:T(1,128)S(1)}, f32[4,1,1024]{2,1,0:T(1,128)S(1)}, u32[]{:S(2)}, u32[]{:S(2)}) collective-permute-start(f32[4,1,1024]{2,1,0:T(1,128)S(1)} %get-tuple-element.42), channel_id=1, source_target_pairs={{0,1},{1,2},{2,3},{4,5},{5,6},{6,7},{8,9},{9,10},{10,11},{12,13},{... | collective-permute-start | bytes 49160 | tf_op jit(solution)/shard_map/ppermute | solution.py:15
  127.0 1.3 collective-permute-start.31
  128.3 4.9 %collective-permute-start.30 = (f32[4,1,1024]{2,1,0:T(1,128)S(1)}, f32[4,1,1024]{2,1,0:T(1,128)S(1)}, u32[]{:S(2)}, u32[]{:S(2)}) collective-permute-start(f32[4,1,1024]{2,1,0:T(1,128)S(1)} %get-tuple-element.40), channel_id=1, source_target_pairs={{0,1},{1,2},{2,3},{4,5},{5,6},{6,7},{8,9},{9,10},{10,11},{12,13},{... | collective-permute-start | bytes 49160 | tf_op jit(solution)/shard_map/ppermute | solution.py:15
  134.3 1.3 collective-permute-start.33
  135.6 4.9 %collective-permute-start.32 = (f32[4,1,1024]{2,1,0:T(1,128)S(1)}, f32[4,1,1024]{2,1,0:T(1,128)S(1)}, u32[]{:S(2)}, u32[]{:S(2)}) collective-permute-start(f32[4,1,1024]{2,1,0:T(1,128)S(1)} %get-tuple-element.38), channel_id=1, source_target_pairs={{0,1},{1,2},{2,3},{4,5},{5,6},{6,7},{8,9},{9,10},{10,11},{12,13},{... | collective-permute-start | bytes 49160 | tf_op jit(solution)/shard_map/ppermute | solution.py:15
  142.9 4.9 %collective-permute-start.34 = (f32[4,1,1024]{2,1,0:T(1,128)S(1)}, f32[4,1,1024]{2,1,0:T(1,128)S(1)}, u32[]{:S(2)}, u32[]{:S(2)}) collective-permute-start(f32[4,1,1024]{2,1,0:T(1,128)S(1)} %get-tuple-element.36), channel_id=1, source_target_pairs={{0,1},{1,2},{2,3},{4,5},{5,6},{6,7},{8,9},{9,10},{10,11},{12,13},{... | collective-permute-start | bytes 49160 | tf_op jit(solution)/shard_map/ppermute | solution.py:15
  150.5 6.3 %all-to-all-start = ((f32[1,8,8192]{2,0,1:T(1,128)}), f32[1,8,8192]{2,0,1:T(1,128)S(1)}, u32[]{:S(2)}, u32[]{:S(2)}) async-start(f32[1,8,8192]{2,0,1:T(1,128)} %all_to_all.27), calls=%async_computation | async-start | bytes 524288 | tf_op jit(solution)/shard_map/all_to_all | solution.py:126
  162.4 1.6 slice.797
  164.0 1.6 slice.806
  165.5 1.6 slice.799
  175.8 1.6 slice.803
  177.4 1.6 slice.801
  181.7 1.6 slice.819
  185.9 6.0 %all-to-all-start.1 = ((f32[8,1,8192]{2,1,0:T(1,128)}), f32[8,1,8192]{2,1,0:T(1,128)S(1)}, u32[]{:S(2)}, u32[]{:S(2)}) async-start(f32[8,1,8192]{2,1,0:T(1,128)} %copy.67), calls=%async_computation.1 | async-start | bytes 524288 | tf_op jit(solution)/shard_map/all_to_all | solution.py:139
  191.9 43.9 %psum.7 = f32[]{:T(128)} all-reduce(f32[]{:T(128)} %get-tuple-element.10), channel_id=1, replica_groups=mesh['tm'=8,'space'=4] {'tm','space'}, use_global_device_ids=true, to_apply=%region_1.2 | all-reduce | flops 1 | bytes 8 | tf_op jit(solution)/shard_map/psum | solution.py:117
  (220 shorter events, 55.0 us)
Async XLA Ops:
  1.6 18.3 %collective-permute-start.1 = (f32[4,1,1024]{2,1,0:T(1,128)S(1)}, f32[4,1,1024]{2,1,0:T(1,128)S(1)}, u32[]{:S(2)}, u32[]{:S(2)}) collective-permute-start(f32[4,1,1024]{2,1,0:T(1,128)S(1)} %get-tuple-element.99), channel_id=1, source_target_pairs={{0,1},{1,2},{2,3},{4,5},{5,6},{6,7},{8,9},{9,10},{10,11},{12,13},{... | collective-permute-start | bytes 49160 | tf_op jit(solution)/shard_map/ppermute | solution.py:15
  4.0 15.9 %collective-permute-start = (f32[4,1,1024]{2,1,0:T(1,128)S(1)}, f32[4,1,1024]{2,1,0:T(1,128)S(1)}, u32[]{:S(2)}, u32[]{:S(2)}) collective-permute-start(f32[4,1,1024]{2,1,0:T(1,128)S(1)} %get-tuple-element.98), channel_id=1, source_target_pairs={{1,0},{2,1},{3,2},{5,4},{6,5},{7,6},{9,8},{10,9},{11,10},{13,12},{... | collective-permute-start | bytes 49160 | tf_op jit(solution)/shard_map/ppermute | solution.py:18
  7.0 12.8 %collective-permute-start.19 = (f32[2,1,1024]{2,1,0:T(1,128)S(1)}, f32[2,1,1024]{2,1,0:T(1,128)S(1)}, u32[]{:S(2)}, u32[]{:S(2)}) collective-permute-start(f32[2,1,1024]{2,1,0:T(1,128)S(1)} %get-tuple-element.115), channel_id=1, source_target_pairs={{1,0},{2,1},{3,2},{5,4},{6,5},{7,6},{9,8},{10,9},{11,10},{13,12},{... | collective-permute-start | bytes 24584 | tf_op jit(solution)/shard_map/ppermute | solution.py:18
  8.3 11.5 %collective-permute-start.18 = (f32[2,1,1024]{2,1,0:T(1,128)S(1)}, f32[2,1,1024]{2,1,0:T(1,128)S(1)}, u32[]{:S(2)}, u32[]{:S(2)}) collective-permute-start(f32[2,1,1024]{2,1,0:T(1,128)S(1)} %get-tuple-element.114), channel_id=1, source_target_pairs={{0,1},{1,2},{2,3},{4,5},{5,6},{6,7},{8,9},{9,10},{10,11},{12,13},{... | collective-permute-start | bytes 24584 | tf_op jit(solution)/shard_map/ppermute | solution.py:15
  17.1 1.8 copy-start.2
  17.1 2.7 %copy-start.1 = (f32[1,16,1024]{2,1,0:T(8,128)S(1)}, f32[1,16,1024]{2,1,0:T(8,128)}, u32[]{:S(2)}) copy-start(f32[1,16,1024]{2,1,0:T(8,128)} %param.10) | copy-start | bytes 196612
  17.1 2.9 %copy-start = (f32[1,4,16,1024]{3,2,1,0:T(8,128)S(1)}, f32[1,4,16,1024]{3,2,1,0:T(8,128)}, u32[]{:S(2)}) copy-start(f32[1,4,16,1024]{3,2,1,0:T(8,128)} %param.8) | copy-start | bytes 786436
  20.3 6.6 %collective-permute-start.3 = (f32[4,1,1024]{2,1,0:T(1,128)S(1)}, f32[4,1,1024]{2,1,0:T(1,128)S(1)}, u32[]{:S(2)}, u32[]{:S(2)}) collective-permute-start(f32[4,1,1024]{2,1,0:T(1,128)S(1)} %get-tuple-element.93), channel_id=1, source_target_pairs={{0,1},{1,2},{2,3},{4,5},{5,6},{6,7},{8,9},{9,10},{10,11},{12,13},{... | collective-permute-start | bytes 49160 | tf_op jit(solution)/shard_map/ppermute | solution.py:15
  24.0 3.1 %collective-permute-start.2 = (f32[4,1,1024]{2,1,0:T(1,128)S(1)}, f32[4,1,1024]{2,1,0:T(1,128)S(1)}, u32[]{:S(2)}, u32[]{:S(2)}) collective-permute-start(f32[4,1,1024]{2,1,0:T(1,128)S(1)} %get-tuple-element.92), channel_id=1, source_target_pairs={{1,0},{2,1},{3,2},{5,4},{6,5},{7,6},{9,8},{10,9},{11,10},{13,12},{... | collective-permute-start | bytes 49160 | tf_op jit(solution)/shard_map/ppermute | solution.py:18
  27.4 7.3 %collective-permute-start.5 = (f32[4,1,1024]{2,1,0:T(1,128)S(1)}, f32[4,1,1024]{2,1,0:T(1,128)S(1)}, u32[]{:S(2)}, u32[]{:S(2)}) collective-permute-start(f32[4,1,1024]{2,1,0:T(1,128)S(1)} %get-tuple-element.87), channel_id=1, source_target_pairs={{0,1},{1,2},{2,3},{4,5},{5,6},{6,7},{8,9},{9,10},{10,11},{12,13},{... | collective-permute-start | bytes 49160 | tf_op jit(solution)/shard_map/ppermute | solution.py:15
  31.8 3.1 %collective-permute-start.4 = (f32[4,1,1024]{2,1,0:T(1,128)S(1)}, f32[4,1,1024]{2,1,0:T(1,128)S(1)}, u32[]{:S(2)}, u32[]{:S(2)}) collective-permute-start(f32[4,1,1024]{2,1,0:T(1,128)S(1)} %get-tuple-element.86), channel_id=1, source_target_pairs={{1,0},{2,1},{3,2},{5,4},{6,5},{7,6},{9,8},{10,9},{11,10},{13,12},{... | collective-permute-start | bytes 49160 | tf_op jit(solution)/shard_map/ppermute | solution.py:18
  35.2 7.1 %collective-permute-start.7 = (f32[4,1,1024]{2,1,0:T(1,128)S(1)}, f32[4,1,1024]{2,1,0:T(1,128)S(1)}, u32[]{:S(2)}, u32[]{:S(2)}) collective-permute-start(f32[4,1,1024]{2,1,0:T(1,128)S(1)} %get-tuple-element.81), channel_id=1, source_target_pairs={{0,1},{1,2},{2,3},{4,5},{5,6},{6,7},{8,9},{9,10},{10,11},{12,13},{... | collective-permute-start | bytes 49160 | tf_op jit(solution)/shard_map/ppermute | solution.py:15
  39.4 3.1 %collective-permute-start.6 = (f32[4,1,1024]{2,1,0:T(1,128)S(1)}, f32[4,1,1024]{2,1,0:T(1,128)S(1)}, u32[]{:S(2)}, u32[]{:S(2)}) collective-permute-start(f32[4,1,1024]{2,1,0:T(1,128)S(1)} %get-tuple-element.80), channel_id=1, source_target_pairs={{1,0},{2,1},{3,2},{5,4},{6,5},{7,6},{9,8},{10,9},{11,10},{13,12},{... | collective-permute-start | bytes 49160 | tf_op jit(solution)/shard_map/ppermute | solution.py:18
  42.8 7.1 %collective-permute-start.9 = (f32[4,1,1024]{2,1,0:T(1,128)S(1)}, f32[4,1,1024]{2,1,0:T(1,128)S(1)}, u32[]{:S(2)}, u32[]{:S(2)}) collective-permute-start(f32[4,1,1024]{2,1,0:T(1,128)S(1)} %get-tuple-element.75), channel_id=1, source_target_pairs={{0,1},{1,2},{2,3},{4,5},{5,6},{6,7},{8,9},{9,10},{10,11},{12,13},{... | collective-permute-start | bytes 49160 | tf_op jit(solution)/shard_map/ppermute | solution.py:15
  46.9 3.1 %collective-permute-start.8 = (f32[4,1,1024]{2,1,0:T(1,128)S(1)}, f32[4,1,1024]{2,1,0:T(1,128)S(1)}, u32[]{:S(2)}, u32[]{:S(2)}) collective-permute-start(f32[4,1,1024]{2,1,0:T(1,128)S(1)} %get-tuple-element.74), channel_id=1, source_target_pairs={{1,0},{2,1},{3,2},{5,4},{6,5},{7,6},{9,8},{10,9},{11,10},{13,12},{... | collective-permute-start | bytes 49160 | tf_op jit(solution)/shard_map/ppermute | solution.py:18
  50.4 7.1 %collective-permute-start.11 = (f32[4,1,1024]{2,1,0:T(1,128)S(1)}, f32[4,1,1024]{2,1,0:T(1,128)S(1)}, u32[]{:S(2)}, u32[]{:S(2)}) collective-permute-start(f32[4,1,1024]{2,1,0:T(1,128)S(1)} %get-tuple-element.69), channel_id=1, source_target_pairs={{0,1},{1,2},{2,3},{4,5},{5,6},{6,7},{8,9},{9,10},{10,11},{12,13},{... | collective-permute-start | bytes 49160 | tf_op jit(solution)/shard_map/ppermute | solution.py:15
  54.5 3.1 %collective-permute-start.10 = (f32[4,1,1024]{2,1,0:T(1,128)S(1)}, f32[4,1,1024]{2,1,0:T(1,128)S(1)}, u32[]{:S(2)}, u32[]{:S(2)}) collective-permute-start(f32[4,1,1024]{2,1,0:T(1,128)S(1)} %get-tuple-element.68), channel_id=1, source_target_pairs={{1,0},{2,1},{3,2},{5,4},{6,5},{7,6},{9,8},{10,9},{11,10},{13,12},{... | collective-permute-start | bytes 49160 | tf_op jit(solution)/shard_map/ppermute | solution.py:18
  57.9 7.3 %collective-permute-start.13 = (f32[4,1,1024]{2,1,0:T(1,128)S(1)}, f32[4,1,1024]{2,1,0:T(1,128)S(1)}, u32[]{:S(2)}, u32[]{:S(2)}) collective-permute-start(f32[4,1,1024]{2,1,0:T(1,128)S(1)} %get-tuple-element.63), channel_id=1, source_target_pairs={{0,1},{1,2},{2,3},{4,5},{5,6},{6,7},{8,9},{9,10},{10,11},{12,13},{... | collective-permute-start | bytes 49160 | tf_op jit(solution)/shard_map/ppermute | solution.py:15
  62.1 3.1 %collective-permute-start.12 = (f32[4,1,1024]{2,1,0:T(1,128)S(1)}, f32[4,1,1024]{2,1,0:T(1,128)S(1)}, u32[]{:S(2)}, u32[]{:S(2)}) collective-permute-start(f32[4,1,1024]{2,1,0:T(1,128)S(1)} %get-tuple-element.62), channel_id=1, source_target_pairs={{1,0},{2,1},{3,2},{5,4},{6,5},{7,6},{9,8},{10,9},{11,10},{13,12},{... | collective-permute-start | bytes 49160 | tf_op jit(solution)/shard_map/ppermute | solution.py:18
  65.5 16.1 %copy-start.4 = (f32[1,4]{1,0:T(1,128)S(1)}, f32[1,4]{1,0:T(1,128)}, u32[]{:S(2)}) copy-start(f32[1,4]{1,0:T(1,128)} %param.14) | copy-start | bytes 52
  65.6 5.5 %collective-permute-start.15 = (f32[4,1,1024]{2,1,0:T(1,128)S(1)}, f32[4,1,1024]{2,1,0:T(1,128)S(1)}, u32[]{:S(2)}, u32[]{:S(2)}) collective-permute-start(f32[4,1,1024]{2,1,0:T(1,128)S(1)} %get-tuple-element.57), channel_id=1, source_target_pairs={{0,1},{1,2},{2,3},{4,5},{5,6},{6,7},{8,9},{9,10},{10,11},{12,13},{... | collective-permute-start | bytes 49160 | tf_op jit(solution)/shard_map/ppermute | solution.py:15
  69.7 3.1 %collective-permute-start.14 = (f32[4,1,1024]{2,1,0:T(1,128)S(1)}, f32[4,1,1024]{2,1,0:T(1,128)S(1)}, u32[]{:S(2)}, u32[]{:S(2)}) collective-permute-start(f32[4,1,1024]{2,1,0:T(1,128)S(1)} %get-tuple-element.56), channel_id=1, source_target_pairs={{1,0},{2,1},{3,2},{5,4},{6,5},{7,6},{9,8},{10,9},{11,10},{13,12},{... | collective-permute-start | bytes 49160 | tf_op jit(solution)/shard_map/ppermute | solution.py:18
  73.0 8.6 %collective-permute-start.16 = (f32[4,16,1024]{2,1,0:T(8,128)S(1)}, f32[4,16,1024]{2,1,0:T(8,128)S(1)}, u32[]{:S(2)}, u32[]{:S(2)}) collective-permute-start(f32[4,16,1024]{2,1,0:T(8,128)S(1)} %fusion.33), channel_id=1, source_target_pairs={{0,4},{4,8},{8,12},{12,16},{16,20},{20,24},{24,28},{1,5},{5,9},{9,... | collective-permute-start | bytes 786440 | tf_op jit(solution)/shard_map/ppermute | solution.py:26
  81.7 10.9 %collective-permute-start.17 = (f32[4,16,1024]{2,1,0:T(8,128)S(1)}, f32[4,16,1024]{2,1,0:T(8,128)S(1)}, u32[]{:S(2)}, u32[]{:S(2)}) collective-permute-start(f32[4,16,1024]{2,1,0:T(8,128)S(1)} %subtract_multiply_fusion), channel_id=1, source_target_pairs={{4,0},{8,4},{12,8},{16,12},{20,16},{24,20},{28,24},{5,1},{9,5},{13... | collective-permute-start | bytes 786440 | tf_op jit(solution)/shard_map/ppermute | solution.py:26
  92.8 4.6 %collective-permute-start.21 = (f32[4,1,1024]{2,1,0:T(1,128)S(1)}, f32[4,1,1024]{2,1,0:T(1,128)S(1)}, u32[]{:S(2)}, u32[]{:S(2)}) collective-permute-start(f32[4,1,1024]{2,1,0:T(1,128)S(1)} %get-tuple-element.51), channel_id=1, source_target_pairs={{1,0},{2,1},{3,2},{5,4},{6,5},{7,6},{9,8},{10,9},{11,10},{13,12},{... | collective-permute-start | bytes 49160 | tf_op jit(solution)/shard_map/ppermute | solution.py:18
  94.1 3.9 %collective-permute-start.20 = (f32[4,1,1024]{2,1,0:T(1,128)S(1)}, f32[4,1,1024]{2,1,0:T(1,128)S(1)}, u32[]{:S(2)}, u32[]{:S(2)}) collective-permute-start(f32[4,1,1024]{2,1,0:T(1,128)S(1)} %get-tuple-element.50), channel_id=1, source_target_pairs={{0,1},{1,2},{2,3},{4,5},{5,6},{6,7},{8,9},{9,10},{10,11},{12,13},{... | collective-permute-start | bytes 49160 | tf_op jit(solution)/shard_map/ppermute | solution.py:15
  98.3 5.8 %collective-permute-start.23 = (f32[4,1,1024]{2,1,0:T(1,128)S(1)}, f32[4,1,1024]{2,1,0:T(1,128)S(1)}, u32[]{:S(2)}, u32[]{:S(2)}) collective-permute-start(f32[4,1,1024]{2,1,0:T(1,128)S(1)} %get-tuple-element.49), channel_id=1, source_target_pairs={{1,0},{2,1},{3,2},{5,4},{6,5},{7,6},{9,8},{10,9},{11,10},{13,12},{... | collective-permute-start | bytes 49160 | tf_op jit(solution)/shard_map/ppermute | solution.py:18
  99.6 5.0 %collective-permute-start.22 = (f32[4,1,1024]{2,1,0:T(1,128)S(1)}, f32[4,1,1024]{2,1,0:T(1,128)S(1)}, u32[]{:S(2)}, u32[]{:S(2)}) collective-permute-start(f32[4,1,1024]{2,1,0:T(1,128)S(1)} %get-tuple-element.48), channel_id=1, source_target_pairs={{0,1},{1,2},{2,3},{4,5},{5,6},{6,7},{8,9},{9,10},{10,11},{12,13},{... | collective-permute-start | bytes 49160 | tf_op jit(solution)/shard_map/ppermute | solution.py:15
  105.0 6.4 %collective-permute-start.25 = (f32[4,1,1024]{2,1,0:T(1,128)S(1)}, f32[4,1,1024]{2,1,0:T(1,128)S(1)}, u32[]{:S(2)}, u32[]{:S(2)}) collective-permute-start(f32[4,1,1024]{2,1,0:T(1,128)S(1)} %get-tuple-element.47), channel_id=1, source_target_pairs={{1,0},{2,1},{3,2},{5,4},{6,5},{7,6},{9,8},{10,9},{11,10},{13,12},{... | collective-permute-start | bytes 49160 | tf_op jit(solution)/shard_map/ppermute | solution.py:18
  106.3 5.7 %collective-permute-start.24 = (f32[4,1,1024]{2,1,0:T(1,128)S(1)}, f32[4,1,1024]{2,1,0:T(1,128)S(1)}, u32[]{:S(2)}, u32[]{:S(2)}) collective-permute-start(f32[4,1,1024]{2,1,0:T(1,128)S(1)} %get-tuple-element.46), channel_id=1, source_target_pairs={{0,1},{1,2},{2,3},{4,5},{5,6},{6,7},{8,9},{9,10},{10,11},{12,13},{... | collective-permute-start | bytes 49160 | tf_op jit(solution)/shard_map/ppermute | solution.py:15
  112.3 6.4 %collective-permute-start.27 = (f32[4,1,1024]{2,1,0:T(1,128)S(1)}, f32[4,1,1024]{2,1,0:T(1,128)S(1)}, u32[]{:S(2)}, u32[]{:S(2)}) collective-permute-start(f32[4,1,1024]{2,1,0:T(1,128)S(1)} %get-tuple-element.45), channel_id=1, source_target_pairs={{1,0},{2,1},{3,2},{5,4},{6,5},{7,6},{9,8},{10,9},{11,10},{13,12},{... | collective-permute-start | bytes 49160 | tf_op jit(solution)/shard_map/ppermute | solution.py:18
  113.6 5.7 %collective-permute-start.26 = (f32[4,1,1024]{2,1,0:T(1,128)S(1)}, f32[4,1,1024]{2,1,0:T(1,128)S(1)}, u32[]{:S(2)}, u32[]{:S(2)}) collective-permute-start(f32[4,1,1024]{2,1,0:T(1,128)S(1)} %get-tuple-element.44), channel_id=1, source_target_pairs={{0,1},{1,2},{2,3},{4,5},{5,6},{6,7},{8,9},{9,10},{10,11},{12,13},{... | collective-permute-start | bytes 49160 | tf_op jit(solution)/shard_map/ppermute | solution.py:15
  119.6 6.4 %collective-permute-start.29 = (f32[4,1,1024]{2,1,0:T(1,128)S(1)}, f32[4,1,1024]{2,1,0:T(1,128)S(1)}, u32[]{:S(2)}, u32[]{:S(2)}) collective-permute-start(f32[4,1,1024]{2,1,0:T(1,128)S(1)} %get-tuple-element.43), channel_id=1, source_target_pairs={{1,0},{2,1},{3,2},{5,4},{6,5},{7,6},{9,8},{10,9},{11,10},{13,12},{... | collective-permute-start | bytes 49160 | tf_op jit(solution)/shard_map/ppermute | solution.py:18
  120.9 5.7 %collective-permute-start.28 = (f32[4,1,1024]{2,1,0:T(1,128)S(1)}, f32[4,1,1024]{2,1,0:T(1,128)S(1)}, u32[]{:S(2)}, u32[]{:S(2)}) collective-permute-start(f32[4,1,1024]{2,1,0:T(1,128)S(1)} %get-tuple-element.42), channel_id=1, source_target_pairs={{0,1},{1,2},{2,3},{4,5},{5,6},{6,7},{8,9},{9,10},{10,11},{12,13},{... | collective-permute-start | bytes 49160 | tf_op jit(solution)/shard_map/ppermute | solution.py:15
  127.0 6.4 %collective-permute-start.31 = (f32[4,1,1024]{2,1,0:T(1,128)S(1)}, f32[4,1,1024]{2,1,0:T(1,128)S(1)}, u32[]{:S(2)}, u32[]{:S(2)}) collective-permute-start(f32[4,1,1024]{2,1,0:T(1,128)S(1)} %get-tuple-element.41), channel_id=1, source_target_pairs={{1,0},{2,1},{3,2},{5,4},{6,5},{7,6},{9,8},{10,9},{11,10},{13,12},{... | collective-permute-start | bytes 49160 | tf_op jit(solution)/shard_map/ppermute | solution.py:18
  128.3 5.7 %collective-permute-start.30 = (f32[4,1,1024]{2,1,0:T(1,128)S(1)}, f32[4,1,1024]{2,1,0:T(1,128)S(1)}, u32[]{:S(2)}, u32[]{:S(2)}) collective-permute-start(f32[4,1,1024]{2,1,0:T(1,128)S(1)} %get-tuple-element.40), channel_id=1, source_target_pairs={{0,1},{1,2},{2,3},{4,5},{5,6},{6,7},{8,9},{9,10},{10,11},{12,13},{... | collective-permute-start | bytes 49160 | tf_op jit(solution)/shard_map/ppermute | solution.py:15
  134.3 6.4 %collective-permute-start.33 = (f32[4,1,1024]{2,1,0:T(1,128)S(1)}, f32[4,1,1024]{2,1,0:T(1,128)S(1)}, u32[]{:S(2)}, u32[]{:S(2)}) collective-permute-start(f32[4,1,1024]{2,1,0:T(1,128)S(1)} %get-tuple-element.39), channel_id=1, source_target_pairs={{1,0},{2,1},{3,2},{5,4},{6,5},{7,6},{9,8},{10,9},{11,10},{13,12},{... | collective-permute-start | bytes 49160 | tf_op jit(solution)/shard_map/ppermute | solution.py:18
  135.6 5.7 %collective-permute-start.32 = (f32[4,1,1024]{2,1,0:T(1,128)S(1)}, f32[4,1,1024]{2,1,0:T(1,128)S(1)}, u32[]{:S(2)}, u32[]{:S(2)}) collective-permute-start(f32[4,1,1024]{2,1,0:T(1,128)S(1)} %get-tuple-element.38), channel_id=1, source_target_pairs={{0,1},{1,2},{2,3},{4,5},{5,6},{6,7},{8,9},{9,10},{10,11},{12,13},{... | collective-permute-start | bytes 49160 | tf_op jit(solution)/shard_map/ppermute | solution.py:15
  141.6 6.4 %collective-permute-start.35 = (f32[4,1,1024]{2,1,0:T(1,128)S(1)}, f32[4,1,1024]{2,1,0:T(1,128)S(1)}, u32[]{:S(2)}, u32[]{:S(2)}) collective-permute-start(f32[4,1,1024]{2,1,0:T(1,128)S(1)} %get-tuple-element.37), channel_id=1, source_target_pairs={{1,0},{2,1},{3,2},{5,4},{6,5},{7,6},{9,8},{10,9},{11,10},{13,12},{... | collective-permute-start | bytes 49160 | tf_op jit(solution)/shard_map/ppermute | solution.py:18
  142.9 5.7 %collective-permute-start.34 = (f32[4,1,1024]{2,1,0:T(1,128)S(1)}, f32[4,1,1024]{2,1,0:T(1,128)S(1)}, u32[]{:S(2)}, u32[]{:S(2)}) collective-permute-start(f32[4,1,1024]{2,1,0:T(1,128)S(1)} %get-tuple-element.36), channel_id=1, source_target_pairs={{0,1},{1,2},{2,3},{4,5},{5,6},{6,7},{8,9},{9,10},{10,11},{12,13},{... | collective-permute-start | bytes 49160 | tf_op jit(solution)/shard_map/ppermute | solution.py:15
  147.9 8.9 %copy-start.3 = (f32[8,4]{0,1:T(4,128)S(1)}, f32[8,4]{0,1:T(4,128)}, u32[]{:S(2)}) copy-start(f32[8,4]{0,1:T(4,128)} %param.15) | copy-start | bytes 388
  150.5 16.6 %all-to-all-start = ((f32[1,8,8192]{2,0,1:T(1,128)}), f32[1,8,8192]{2,0,1:T(1,128)S(1)}, u32[]{:S(2)}, u32[]{:S(2)}) async-start(f32[1,8,8192]{2,0,1:T(1,128)} %all_to_all.27), calls=%async_computation | async-start | bytes 524288 | tf_op jit(solution)/shard_map/all_to_all | solution.py:126
  185.9 50.6 %all-to-all-start.1 = ((f32[8,1,8192]{2,1,0:T(1,128)}), f32[8,1,8192]{2,1,0:T(1,128)S(1)}, u32[]{:S(2)}, u32[]{:S(2)}) async-start(f32[8,1,8192]{2,1,0:T(1,128)} %copy.67), calls=%async_computation.1 | async-start | bytes 524288 | tf_op jit(solution)/shard_map/all_to_all | solution.py:139
where the time goes:
time: 241 us; the launch traced here: 239 us
  starting transfers between devices  112 us (46%)
  blocking collectives  43.9 us (18%)
  local copies, waits for them, and re-layouts  37.5 us (16%)
  waiting for transfers between devices  18.6 us (8%)
  matrix products  13.5 us (6%)
  other arithmetic  8.53 us (4%)
  between operations  4.62 us (2%)
    ppermute x17, starting transfers between devices, padded_2(): lax.ppermute(lax.slice_in_dim(block, block.shape[dim] - width, None, axis...  73.3 us
    psum x1, blocking collectives, on_device(): square_sum = lax.psum(jnp.sum(gradient * gradient), ('tm', 'space'))  43.9 us
    ppermute x17, starting transfers between devices, padded_2(): lax.ppermute(lax.slice_in_dim(block, 0, width, axis=dim), axis, backward)  22.1 us
    slice x17, local copies, waits for them, and re-layouts, on_device(): lax.associative_scan(combine, (next_cols, inno_cols * forward_cols), reve...  16.4 us
    ppermute x2, waiting for transfers between devices, passed_along(): lax.ppermute(value, axis, [(source, source + steps) for source in range(l...  11.7 us
    dot_general x8, matrix products, select_rows(): jnp.einsum('kb,cbrx->kcrx', picker, blocks, precision=lax.Precision.HIGHEST)  7.44 us
    slice x11, local copies, waits for them, and re-layouts, on_device(): lax.associative_scan(combine, (rate_cols, inno_cols * columns), axis=0)[1]  7.18 us
    all_to_all x1, starting transfers between devices, on_device(): lax.all_to_all(flat_grad, 'tm', split_axis=1, concat_axis=0, tiled=True)  6.3 us
  transfers between devices with their start and end apart: 38, of which 16 were waited for; matrix products, arithmetic and copies ran while one was open for 13% of the time, Pallas kernels for 0%

commit v1 on v0

--- a/solution.py
+++ b/solution.py
@@ -123,7 +123,9 @@
     next_rates = jnp.concatenate([rates[1:], jnp.zeros((1, rates.shape[1]), jnp.float32)], axis=0)
     column_count = gradient.size // windows
     flat_grad = gradient.reshape(1, gradient.size)
-    columns = lax.all_to_all(flat_grad, "tm", split_axis=1, concat_axis=0, tiled=True)
+    cells = jnp.split(flat_grad, lax.axis_size("tm"), axis=1)
+    incoming = lax.all_to_all(jnp.stack(cells), "tm", 0, 0)
+    columns = jnp.concatenate(incoming, axis=0)
     places = position * column_count + jnp.arange(column_count, dtype=jnp.int32)
     member = places // (field_shape[1] * field_shape[2])
     onehot = (member[None, :] == jnp.arange(field_shape[0], dtype=jnp.int32)[:, None]).astype(

time: 241 us -> 245 us (1.017)
  local copies, waits for them, and re-layouts: 37.5 us -> 41.7 us
    unnamed x10 -> x17, local copies, waits for them, and re-layouts: 0.03 us -> 4.35 us
where the time goes in v1:
time: 245 us; the launch traced here: 243 us
  starting transfers between devices  112 us (46%)
  blocking collectives  43.9 us (18%)
  local copies, waits for them, and re-layouts  41.7 us (17%)
  waiting for transfers between devices  18.6 us (8%)
  matrix products  13.5 us (6%)
  other arithmetic  8.53 us (3%)
  between operations  4.62 us (2%)
    ppermute x17, starting transfers between devices, padded_2(): lax.ppermute(lax.slice_in_dim(block, block.shape[dim] - width, None, axis...  73.3 us
    psum x1, blocking collectives, on_device(): square_sum = lax.psum(jnp.sum(gradient * gradient), ('tm', 'space'))  43.9 us
    ppermute x17, starting transfers between devices, padded_2(): lax.ppermute(lax.slice_in_dim(block, 0, width, axis=dim), axis, backward)  22.1 us
    slice x17, local copies, waits for them, and re-layouts, on_device(): lax.associative_scan(combine, (next_cols, inno_cols * forward_cols), reve...  16.4 us
    ppermute x2, waiting for transfers between devices, passed_along(): lax.ppermute(value, axis, [(source, source + steps) for source in range(l...  11.7 us
    dot_general x8, matrix products, select_rows(): jnp.einsum('kb,cbrx->kcrx', picker, blocks, precision=lax.Precision.HIGHEST)  7.44 us
    slice x11, local copies, waits for them, and re-layouts, on_device(): lax.associative_scan(combine, (rate_cols, inno_cols * columns), axis=0)[1]  7.18 us
    all_to_all x1, starting transfers between devices, on_device(): incoming = lax.all_to_all(jnp.stack(cells), 'tm', 0, 0)  6.3 us
  transfers between devices with their start and end apart: 38, of which 16 were waited for; matrix products, arithmetic and copies ran while one was open for 13% of the time, Pallas kernels for 0%

profile of v1, /device:TPU:0, one launch (start us, length us, event | category | flops | bytes accessed | tf_op | source)
XLA Modules:
  0.0 243.3 jit_solution(3427168214540678982)
XLA Ops:
  1.6 2.4 collective-permute-start.1
  4.0 1.3 collective-permute-start
  7.0 1.3 collective-permute-start.19
  8.3 5.8 %collective-permute-start.18 = (f32[2,1,1024]{2,1,0:T(1,128)S(1)}, f32[2,1,1024]{2,1,0:T(1,128)S(1)}, u32[]{:S(2)}, u32[]{:S(2)}) collective-permute-start(f32[2,1,1024]{2,1,0:T(1,128)S(1)} %get-tuple-element.114), channel_id=1, source_target_pairs={{0,1},{1,2},{2,3},{4,5},{5,6},{6,7},{8,9},{9,10},{10,11},{12,13},{... | collective-permute-start | bytes 24584 | tf_op jit(solution)/shard_map/ppermute | solution.py:15
  17.1 1.7 fusion.169
  20.3 3.6 %collective-permute-start.3 = (f32[4,1,1024]{2,1,0:T(1,128)S(1)}, f32[4,1,1024]{2,1,0:T(1,128)S(1)}, u32[]{:S(2)}, u32[]{:S(2)}) collective-permute-start(f32[4,1,1024]{2,1,0:T(1,128)S(1)} %get-tuple-element.93), channel_id=1, source_target_pairs={{0,1},{1,2},{2,3},{4,5},{5,6},{6,7},{8,9},{9,10},{10,11},{12,13},{... | collective-permute-start | bytes 49160 | tf_op jit(solution)/shard_map/ppermute | solution.py:15
  24.0 1.3 collective-permute-start.2
  27.4 4.4 %collective-permute-start.5 = (f32[4,1,1024]{2,1,0:T(1,128)S(1)}, f32[4,1,1024]{2,1,0:T(1,128)S(1)}, u32[]{:S(2)}, u32[]{:S(2)}) collective-permute-start(f32[4,1,1024]{2,1,0:T(1,128)S(1)} %get-tuple-element.87), channel_id=1, source_target_pairs={{0,1},{1,2},{2,3},{4,5},{5,6},{6,7},{8,9},{9,10},{10,11},{12,13},{... | collective-permute-start | bytes 49160 | tf_op jit(solution)/shard_map/ppermute | solution.py:15
  31.8 1.3 collective-permute-start.4
  35.2 4.2 %collective-permute-start.7 = (f32[4,1,1024]{2,1,0:T(1,128)S(1)}, f32[4,1,1024]{2,1,0:T(1,128)S(1)}, u32[]{:S(2)}, u32[]{:S(2)}) collective-permute-start(f32[4,1,1024]{2,1,0:T(1,128)S(1)} %get-tuple-element.81), channel_id=1, source_target_pairs={{0,1},{1,2},{2,3},{4,5},{5,6},{6,7},{8,9},{9,10},{10,11},{12,13},{... | collective-permute-start | bytes 49160 | tf_op jit(solution)/shard_map/ppermute | solution.py:15
  39.4 1.3 collective-permute-start.6
  42.8 4.2 %collective-permute-start.9 = (f32[4,1,1024]{2,1,0:T(1,128)S(1)}, f32[4,1,1024]{2,1,0:T(1,128)S(1)}, u32[]{:S(2)}, u32[]{:S(2)}) collective-permute-start(f32[4,1,1024]{2,1,0:T(1,128)S(1)} %get-tuple-element.75), channel_id=1, source_target_pairs={{0,1},{1,2},{2,3},{4,5},{5,6},{6,7},{8,9},{9,10},{10,11},{12,13},{... | collective-permute-start | bytes 49160 | tf_op jit(solution)/shard_map/ppermute | solution.py:15
  46.9 1.3 collective-permute-start.8
  50.4 4.2 %collective-permute-start.11 = (f32[4,1,1024]{2,1,0:T(1,128)S(1)}, f32[4,1,1024]{2,1,0:T(1,128)S(1)}, u32[]{:S(2)}, u32[]{:S(2)}) collective-permute-start(f32[4,1,1024]{2,1,0:T(1,128)S(1)} %get-tuple-element.69), channel_id=1, source_target_pairs={{0,1},{1,2},{2,3},{4,5},{5,6},{6,7},{8,9},{9,10},{10,11},{12,13},{... | collective-permute-start | bytes 49160 | tf_op jit(solution)/shard_map/ppermute | solution.py:15
  54.5 1.3 collective-permute-start.10
  57.9 4.2 %collective-permute-start.13 = (f32[4,1,1024]{2,1,0:T(1,128)S(1)}, f32[4,1,1024]{2,1,0:T(1,128)S(1)}, u32[]{:S(2)}, u32[]{:S(2)}) collective-permute-start(f32[4,1,1024]{2,1,0:T(1,128)S(1)} %get-tuple-element.63), channel_id=1, source_target_pairs={{0,1},{1,2},{2,3},{4,5},{5,6},{6,7},{8,9},{9,10},{10,11},{12,13},{... | collective-permute-start | bytes 49160 | tf_op jit(solution)/shard_map/ppermute | solution.py:15
  62.1 1.5 collective-permute-start.12
  65.6 4.1 %collective-permute-start.15 = (f32[4,1,1024]{2,1,0:T(1,128)S(1)}, f32[4,1,1024]{2,1,0:T(1,128)S(1)}, u32[]{:S(2)}, u32[]{:S(2)}) collective-permute-start(f32[4,1,1024]{2,1,0:T(1,128)S(1)} %get-tuple-element.57), channel_id=1, source_target_pairs={{0,1},{1,2},{2,3},{4,5},{5,6},{6,7},{8,9},{9,10},{10,11},{12,13},{... | collective-permute-start | bytes 49160 | tf_op jit(solution)/shard_map/ppermute | solution.py:15
  69.7 1.3 collective-permute-start.14
  71.1 1.7 collective-permute-done.14
  73.0 3.4 %collective-permute-start.16 = (f32[4,16,1024]{2,1,0:T(8,128)S(1)}, f32[4,16,1024]{2,1,0:T(8,128)S(1)}, u32[]{:S(2)}, u32[]{:S(2)}) collective-permute-start(f32[4,16,1024]{2,1,0:T(8,128)S(1)} %fusion.33), channel_id=1, source_target_pairs={{0,4},{4,8},{8,12},{12,16},{16,20},{20,24},{24,28},{1,5},{5,9},{9,... | collective-permute-start | bytes 786440 | tf_op jit(solution)/shard_map/ppermute | solution.py:26
  78.0 3.6 %collective-permute-done.16 = f32[4,16,1024]{2,1,0:T(8,128)S(1)} collective-permute-done((f32[4,16,1024]{2,1,0:T(8,128)S(1)}, f32[4,16,1024]{2,1,0:T(8,128)S(1)}, u32[]{:S(2)}, u32[]{:S(2)}) %collective-permute-start.16) | collective-permute-done | bytes 262176 | tf_op jit(solution)/shard_map/ppermute | solution.py:26
  81.7 1.3 collective-permute-start.17
  84.6 8.1 %collective-permute-done.17 = f32[4,16,1024]{2,1,0:T(8,128)S(1)} collective-permute-done((f32[4,16,1024]{2,1,0:T(8,128)S(1)}, f32[4,16,1024]{2,1,0:T(8,128)S(1)}, u32[]{:S(2)}, u32[]{:S(2)}) %collective-permute-start.17) | collective-permute-done | bytes 262176 | tf_op jit(solution)/shard_map/ppermute | solution.py:26
  92.8 1.3 collective-permute-start.21
  94.1 3.0 %collective-permute-start.20 = (f32[4,1,1024]{2,1,0:T(1,128)S(1)}, f32[4,1,1024]{2,1,0:T(1,128)S(1)}, u32[]{:S(2)}, u32[]{:S(2)}) collective-permute-start(f32[4,1,1024]{2,1,0:T(1,128)S(1)} %get-tuple-element.50), channel_id=1, source_target_pairs={{0,1},{1,2},{2,3},{4,5},{5,6},{6,7},{8,9},{9,10},{10,11},{12,13},{... | collective-permute-start | bytes 49160 | tf_op jit(solution)/shard_map/ppermute | solution.py:15
  98.3 1.3 collective-permute-start.23
  99.6 4.2 %collective-permute-start.22 = (f32[4,1,1024]{2,1,0:T(1,128)S(1)}, f32[4,1,1024]{2,1,0:T(1,128)S(1)}, u32[]{:S(2)}, u32[]{:S(2)}) collective-permute-start(f32[4,1,1024]{2,1,0:T(1,128)S(1)} %get-tuple-element.48), channel_id=1, source_target_pairs={{0,1},{1,2},{2,3},{4,5},{5,6},{6,7},{8,9},{9,10},{10,11},{12,13},{... | collective-permute-start | bytes 49160 | tf_op jit(solution)/shard_map/ppermute | solution.py:15
  105.0 1.3 collective-permute-start.25
  106.3 4.9 %collective-permute-start.24 = (f32[4,1,1024]{2,1,0:T(1,128)S(1)}, f32[4,1,1024]{2,1,0:T(1,128)S(1)}, u32[]{:S(2)}, u32[]{:S(2)}) collective-permute-start(f32[4,1,1024]{2,1,0:T(1,128)S(1)} %get-tuple-element.46), channel_id=1, source_target_pairs={{0,1},{1,2},{2,3},{4,5},{5,6},{6,7},{8,9},{9,10},{10,11},{12,13},{... | collective-permute-start | bytes 49160 | tf_op jit(solution)/shard_map/ppermute | solution.py:15
  112.3 1.3 collective-permute-start.27
  113.6 4.9 %collective-permute-start.26 = (f32[4,1,1024]{2,1,0:T(1,128)S(1)}, f32[4,1,1024]{2,1,0:T(1,128)S(1)}, u32[]{:S(2)}, u32[]{:S(2)}) collective-permute-start(f32[4,1,1024]{2,1,0:T(1,128)S(1)} %get-tuple-element.44), channel_id=1, source_target_pairs={{0,1},{1,2},{2,3},{4,5},{5,6},{6,7},{8,9},{9,10},{10,11},{12,13},{... | collective-permute-start | bytes 49160 | tf_op jit(solution)/shard_map/ppermute | solution.py:15
  119.6 1.3 collective-permute-start.29
  120.9 4.9 %collective-permute-start.28 = (f32[4,1,1024]{2,1,0:T(1,128)S(1)}, f32[4,1,1024]{2,1,0:T(1,128)S(1)}, u32[]{:S(2)}, u32[]{:S(2)}) collective-permute-start(f32[4,1,1024]{2,1,0:T(1,128)S(1)} %get-tuple-element.42), channel_id=1, source_target_pairs={{0,1},{1,2},{2,3},{4,5},{5,6},{6,7},{8,9},{9,10},{10,11},{12,13},{... | collective-permute-start | bytes 49160 | tf_op jit(solution)/shard_map/ppermute | solution.py:15
  127.0 1.3 collective-permute-start.31
  128.3 4.9 %collective-permute-start.30 = (f32[4,1,1024]{2,1,0:T(1,128)S(1)}, f32[4,1,1024]{2,1,0:T(1,128)S(1)}, u32[]{:S(2)}, u32[]{:S(2)}) collective-permute-start(f32[4,1,1024]{2,1,0:T(1,128)S(1)} %get-tuple-element.40), channel_id=1, source_target_pairs={{0,1},{1,2},{2,3},{4,5},{5,6},{6,7},{8,9},{9,10},{10,11},{12,13},{... | collective-permute-start | bytes 49160 | tf_op jit(solution)/shard_map/ppermute | solution.py:15
  134.3 1.3 collective-permute-start.33
  135.6 4.9 %collective-permute-start.32 = (f32[4,1,1024]{2,1,0:T(1,128)S(1)}, f32[4,1,1024]{2,1,0:T(1,128)S(1)}, u32[]{:S(2)}, u32[]{:S(2)}) collective-permute-start(f32[4,1,1024]{2,1,0:T(1,128)S(1)} %get-tuple-element.38), channel_id=1, source_target_pairs={{0,1},{1,2},{2,3},{4,5},{5,6},{6,7},{8,9},{9,10},{10,11},{12,13},{... | collective-permute-start | bytes 49160 | tf_op jit(solution)/shard_map/ppermute | solution.py:15
  142.9 4.9 %collective-permute-start.34 = (f32[4,1,1024]{2,1,0:T(1,128)S(1)}, f32[4,1,1024]{2,1,0:T(1,128)S(1)}, u32[]{:S(2)}, u32[]{:S(2)}) collective-permute-start(f32[4,1,1024]{2,1,0:T(1,128)S(1)} %get-tuple-element.36), channel_id=1, source_target_pairs={{0,1},{1,2},{2,3},{4,5},{5,6},{6,7},{8,9},{9,10},{10,11},{12,13},{... | collective-permute-start | bytes 49160 | tf_op jit(solution)/shard_map/ppermute | solution.py:15
  154.7 6.3 %all-to-all-start = ((f32[8,1,8192]{2,1,0:T(1,128)}), f32[8,1,8192]{2,1,0:T(1,128)S(1)}, u32[]{:S(2)}, u32[]{:S(2)}) async-start(f32[8,1,8192]{2,1,0:T(1,128)} %fusion.112), calls=%async_computation | async-start | bytes 524288 | tf_op jit(solution)/shard_map/all_to_all | solution.py:127
  166.6 1.6 slice.797
  168.2 1.6 slice.806
  169.8 1.6 slice.799
  180.1 1.6 slice.803
  181.6 1.6 slice.801
  185.9 1.6 slice.819
  190.1 6.0 %all-to-all-start.1 = ((f32[8,1,8192]{2,1,0:T(1,128)}), f32[8,1,8192]{2,1,0:T(1,128)S(1)}, u32[]{:S(2)}, u32[]{:S(2)}) async-start(f32[8,1,8192]{2,1,0:T(1,128)} %copy.66), calls=%async_computation.1 | async-start | bytes 524288 | tf_op jit(solution)/shard_map/all_to_all | solution.py:141
  196.1 43.9 %psum.7 = f32[]{:T(128)} all-reduce(f32[]{:T(128)} %get-tuple-element.10), channel_id=1, replica_groups=mesh['tm'=8,'space'=4] {'tm','space'}, use_global_device_ids=true, to_apply=%region_1.2 | all-reduce | flops 1 | bytes 8 | tf_op jit(solution)/shard_map/psum | solution.py:117
  (228 shorter events, 59.2 us)
Async XLA Ops:
  1.6 18.3 %collective-permute-start.1 = (f32[4,1,1024]{2,1,0:T(1,128)S(1)}, f32[4,1,1024]{2,1,0:T(1,128)S(1)}, u32[]{:S(2)}, u32[]{:S(2)}) collective-permute-start(f32[4,1,1024]{2,1,0:T(1,128)S(1)} %get-tuple-element.99), channel_id=1, source_target_pairs={{0,1},{1,2},{2,3},{4,5},{5,6},{6,7},{8,9},{9,10},{10,11},{12,13},{... | collective-permute-start | bytes 49160 | tf_op jit(solution)/shard_map/ppermute | solution.py:15
  4.0 15.9 %collective-permute-start = (f32[4,1,1024]{2,1,0:T(1,128)S(1)}, f32[4,1,1024]{2,1,0:T(1,128)S(1)}, u32[]{:S(2)}, u32[]{:S(2)}) collective-permute-start(f32[4,1,1024]{2,1,0:T(1,128)S(1)} %get-tuple-element.98), channel_id=1, source_target_pairs={{1,0},{2,1},{3,2},{5,4},{6,5},{7,6},{9,8},{10,9},{11,10},{13,12},{... | collective-permute-start | bytes 49160 | tf_op jit(solution)/shard_map/ppermute | solution.py:18
  7.0 12.8 %collective-permute-start.19 = (f32[2,1,1024]{2,1,0:T(1,128)S(1)}, f32[2,1,1024]{2,1,0:T(1,128)S(1)}, u32[]{:S(2)}, u32[]{:S(2)}) collective-permute-start(f32[2,1,1024]{2,1,0:T(1,128)S(1)} %get-tuple-element.115), channel_id=1, source_target_pairs={{1,0},{2,1},{3,2},{5,4},{6,5},{7,6},{9,8},{10,9},{11,10},{13,12},{... | collective-permute-start | bytes 24584 | tf_op jit(solution)/shard_map/ppermute | solution.py:18
  8.3 11.5 %collective-permute-start.18 = (f32[2,1,1024]{2,1,0:T(1,128)S(1)}, f32[2,1,1024]{2,1,0:T(1,128)S(1)}, u32[]{:S(2)}, u32[]{:S(2)}) collective-permute-start(f32[2,1,1024]{2,1,0:T(1,128)S(1)} %get-tuple-element.114), channel_id=1, source_target_pairs={{0,1},{1,2},{2,3},{4,5},{5,6},{6,7},{8,9},{9,10},{10,11},{12,13},{... | collective-permute-start | bytes 24584 | tf_op jit(solution)/shard_map/ppermute | solution.py:15
  17.1 1.8 copy-start.2
  17.1 2.7 %copy-start.1 = (f32[1,16,1024]{2,1,0:T(8,128)S(1)}, f32[1,16,1024]{2,1,0:T(8,128)}, u32[]{:S(2)}) copy-start(f32[1,16,1024]{2,1,0:T(8,128)} %param.10) | copy-start | bytes 196612
  17.1 2.9 %copy-start = (f32[1,4,16,1024]{3,2,1,0:T(8,128)S(1)}, f32[1,4,16,1024]{3,2,1,0:T(8,128)}, u32[]{:S(2)}) copy-start(f32[1,4,16,1024]{3,2,1,0:T(8,128)} %param.8) | copy-start | bytes 786436
  20.3 6.6 %collective-permute-start.3 = (f32[4,1,1024]{2,1,0:T(1,128)S(1)}, f32[4,1,1024]{2,1,0:T(1,128)S(1)}, u32[]{:S(2)}, u32[]{:S(2)}) collective-permute-start(f32[4,1,1024]{2,1,0:T(1,128)S(1)} %get-tuple-element.93), channel_id=1, source_target_pairs={{0,1},{1,2},{2,3},{4,5},{5,6},{6,7},{8,9},{9,10},{10,11},{12,13},{... | collective-permute-start | bytes 49160 | tf_op jit(solution)/shard_map/ppermute | solution.py:15
  24.0 3.1 %collective-permute-start.2 = (f32[4,1,1024]{2,1,0:T(1,128)S(1)}, f32[4,1,1024]{2,1,0:T(1,128)S(1)}, u32[]{:S(2)}, u32[]{:S(2)}) collective-permute-start(f32[4,1,1024]{2,1,0:T(1,128)S(1)} %get-tuple-element.92), channel_id=1, source_target_pairs={{1,0},{2,1},{3,2},{5,4},{6,5},{7,6},{9,8},{10,9},{11,10},{13,12},{... | collective-permute-start | bytes 49160 | tf_op jit(solution)/shard_map/ppermute | solution.py:18
  27.4 7.3 %collective-permute-start.5 = (f32[4,1,1024]{2,1,0:T(1,128)S(1)}, f32[4,1,1024]{2,1,0:T(1,128)S(1)}, u32[]{:S(2)}, u32[]{:S(2)}) collective-permute-start(f32[4,1,1024]{2,1,0:T(1,128)S(1)} %get-tuple-element.87), channel_id=1, source_target_pairs={{0,1},{1,2},{2,3},{4,5},{5,6},{6,7},{8,9},{9,10},{10,11},{12,13},{... | collective-permute-start | bytes 49160 | tf_op jit(solution)/shard_map/ppermute | solution.py:15
  31.8 3.1 %collective-permute-start.4 = (f32[4,1,1024]{2,1,0:T(1,128)S(1)}, f32[4,1,1024]{2,1,0:T(1,128)S(1)}, u32[]{:S(2)}, u32[]{:S(2)}) collective-permute-start(f32[4,1,1024]{2,1,0:T(1,128)S(1)} %get-tuple-element.86), channel_id=1, source_target_pairs={{1,0},{2,1},{3,2},{5,4},{6,5},{7,6},{9,8},{10,9},{11,10},{13,12},{... | collective-permute-start | bytes 49160 | tf_op jit(solution)/shard_map/ppermute | solution.py:18
  35.2 7.1 %collective-permute-start.7 = (f32[4,1,1024]{2,1,0:T(1,128)S(1)}, f32[4,1,1024]{2,1,0:T(1,128)S(1)}, u32[]{:S(2)}, u32[]{:S(2)}) collective-permute-start(f32[4,1,1024]{2,1,0:T(1,128)S(1)} %get-tuple-element.81), channel_id=1, source_target_pairs={{0,1},{1,2},{2,3},{4,5},{5,6},{6,7},{8,9},{9,10},{10,11},{12,13},{... | collective-permute-start | bytes 49160 | tf_op jit(solution)/shard_map/ppermute | solution.py:15
  39.4 3.1 %collective-permute-start.6 = (f32[4,1,1024]{2,1,0:T(1,128)S(1)}, f32[4,1,1024]{2,1,0:T(1,128)S(1)}, u32[]{:S(2)}, u32[]{:S(2)}) collective-permute-start(f32[4,1,1024]{2,1,0:T(1,128)S(1)} %get-tuple-element.80), channel_id=1, source_target_pairs={{1,0},{2,1},{3,2},{5,4},{6,5},{7,6},{9,8},{10,9},{11,10},{13,12},{... | collective-permute-start | bytes 49160 | tf_op jit(solution)/shard_map/ppermute | solution.py:18
  42.8 7.1 %collective-permute-start.9 = (f32[4,1,1024]{2,1,0:T(1,128)S(1)}, f32[4,1,1024]{2,1,0:T(1,128)S(1)}, u32[]{:S(2)}, u32[]{:S(2)}) collective-permute-start(f32[4,1,1024]{2,1,0:T(1,128)S(1)} %get-tuple-element.75), channel_id=1, source_target_pairs={{0,1},{1,2},{2,3},{4,5},{5,6},{6,7},{8,9},{9,10},{10,11},{12,13},{... | collective-permute-start | bytes 49160 | tf_op jit(solution)/shard_map/ppermute | solution.py:15
  46.9 3.1 %collective-permute-start.8 = (f32[4,1,1024]{2,1,0:T(1,128)S(1)}, f32[4,1,1024]{2,1,0:T(1,128)S(1)}, u32[]{:S(2)}, u32[]{:S(2)}) collective-permute-start(f32[4,1,1024]{2,1,0:T(1,128)S(1)} %get-tuple-element.74), channel_id=1, source_target_pairs={{1,0},{2,1},{3,2},{5,4},{6,5},{7,6},{9,8},{10,9},{11,10},{13,12},{... | collective-permute-start | bytes 49160 | tf_op jit(solution)/shard_map/ppermute | solution.py:18
  50.4 7.1 %collective-permute-start.11 = (f32[4,1,1024]{2,1,0:T(1,128)S(1)}, f32[4,1,1024]{2,1,0:T(1,128)S(1)}, u32[]{:S(2)}, u32[]{:S(2)}) collective-permute-start(f32[4,1,1024]{2,1,0:T(1,128)S(1)} %get-tuple-element.69), channel_id=1, source_target_pairs={{0,1},{1,2},{2,3},{4,5},{5,6},{6,7},{8,9},{9,10},{10,11},{12,13},{... | collective-permute-start | bytes 49160 | tf_op jit(solution)/shard_map/ppermute | solution.py:15
  54.5 3.1 %collective-permute-start.10 = (f32[4,1,1024]{2,1,0:T(1,128)S(1)}, f32[4,1,1024]{2,1,0:T(1,128)S(1)}, u32[]{:S(2)}, u32[]{:S(2)}) collective-permute-start(f32[4,1,1024]{2,1,0:T(1,128)S(1)} %get-tuple-element.68), channel_id=1, source_target_pairs={{1,0},{2,1},{3,2},{5,4},{6,5},{7,6},{9,8},{10,9},{11,10},{13,12},{... | collective-permute-start | bytes 49160 | tf_op jit(solution)/shard_map/ppermute | solution.py:18
  57.9 7.3 %collective-permute-start.13 = (f32[4,1,1024]{2,1,0:T(1,128)S(1)}, f32[4,1,1024]{2,1,0:T(1,128)S(1)}, u32[]{:S(2)}, u32[]{:S(2)}) collective-permute-start(f32[4,1,1024]{2,1,0:T(1,128)S(1)} %get-tuple-element.63), channel_id=1, source_target_pairs={{0,1},{1,2},{2,3},{4,5},{5,6},{6,7},{8,9},{9,10},{10,11},{12,13},{... | collective-permute-start | bytes 49160 | tf_op jit(solution)/shard_map/ppermute | solution.py:15
  62.1 3.1 %collective-permute-start.12 = (f32[4,1,1024]{2,1,0:T(1,128)S(1)}, f32[4,1,1024]{2,1,0:T(1,128)S(1)}, u32[]{:S(2)}, u32[]{:S(2)}) collective-permute-start(f32[4,1,1024]{2,1,0:T(1,128)S(1)} %get-tuple-element.62), channel_id=1, source_target_pairs={{1,0},{2,1},{3,2},{5,4},{6,5},{7,6},{9,8},{10,9},{11,10},{13,12},{... | collective-permute-start | bytes 49160 | tf_op jit(solution)/shard_map/ppermute | solution.py:18
  65.5 16.1 %copy-start.4 = (f32[1,4]{1,0:T(1,128)S(1)}, f32[1,4]{1,0:T(1,128)}, u32[]{:S(2)}) copy-start(f32[1,4]{1,0:T(1,128)} %param.14) | copy-start | bytes 52
  65.6 5.5 %collective-permute-start.15 = (f32[4,1,1024]{2,1,0:T(1,128)S(1)}, f32[4,1,1024]{2,1,0:T(1,128)S(1)}, u32[]{:S(2)}, u32[]{:S(2)}) collective-permute-start(f32[4,1,1024]{2,1,0:T(1,128)S(1)} %get-tuple-element.57), channel_id=1, source_target_pairs={{0,1},{1,2},{2,3},{4,5},{5,6},{6,7},{8,9},{9,10},{10,11},{12,13},{... | collective-permute-start | bytes 49160 | tf_op jit(solution)/shard_map/ppermute | solution.py:15
  69.7 3.1 %collective-permute-start.14 = (f32[4,1,1024]{2,1,0:T(1,128)S(1)}, f32[4,1,1024]{2,1,0:T(1,128)S(1)}, u32[]{:S(2)}, u32[]{:S(2)}) collective-permute-start(f32[4,1,1024]{2,1,0:T(1,128)S(1)} %get-tuple-element.56), channel_id=1, source_target_pairs={{1,0},{2,1},{3,2},{5,4},{6,5},{7,6},{9,8},{10,9},{11,10},{13,12},{... | collective-permute-start | bytes 49160 | tf_op jit(solution)/shard_map/ppermute | solution.py:18
  73.0 8.6 %collective-permute-start.16 = (f32[4,16,1024]{2,1,0:T(8,128)S(1)}, f32[4,16,1024]{2,1,0:T(8,128)S(1)}, u32[]{:S(2)}, u32[]{:S(2)}) collective-permute-start(f32[4,16,1024]{2,1,0:T(8,128)S(1)} %fusion.33), channel_id=1, source_target_pairs={{0,4},{4,8},{8,12},{12,16},{16,20},{20,24},{24,28},{1,5},{5,9},{9,... | collective-permute-start | bytes 786440 | tf_op jit(solution)/shard_map/ppermute | solution.py:26
  81.7 10.9 %collective-permute-start.17 = (f32[4,16,1024]{2,1,0:T(8,128)S(1)}, f32[4,16,1024]{2,1,0:T(8,128)S(1)}, u32[]{:S(2)}, u32[]{:S(2)}) collective-permute-start(f32[4,16,1024]{2,1,0:T(8,128)S(1)} %subtract_multiply_fusion), channel_id=1, source_target_pairs={{4,0},{8,4},{12,8},{16,12},{20,16},{24,20},{28,24},{5,1},{9,5},{13... | collective-permute-start | bytes 786440 | tf_op jit(solution)/shard_map/ppermute | solution.py:26
  92.8 4.6 %collective-permute-start.21 = (f32[4,1,1024]{2,1,0:T(1,128)S(1)}, f32[4,1,1024]{2,1,0:T(1,128)S(1)}, u32[]{:S(2)}, u32[]{:S(2)}) collective-permute-start(f32[4,1,1024]{2,1,0:T(1,128)S(1)} %get-tuple-element.51), channel_id=1, source_target_pairs={{1,0},{2,1},{3,2},{5,4},{6,5},{7,6},{9,8},{10,9},{11,10},{13,12},{... | collective-permute-start | bytes 49160 | tf_op jit(solution)/shard_map/ppermute | solution.py:18
  94.1 3.9 %collective-permute-start.20 = (f32[4,1,1024]{2,1,0:T(1,128)S(1)}, f32[4,1,1024]{2,1,0:T(1,128)S(1)}, u32[]{:S(2)}, u32[]{:S(2)}) collective-permute-start(f32[4,1,1024]{2,1,0:T(1,128)S(1)} %get-tuple-element.50), channel_id=1, source_target_pairs={{0,1},{1,2},{2,3},{4,5},{5,6},{6,7},{8,9},{9,10},{10,11},{12,13},{... | collective-permute-start | bytes 49160 | tf_op jit(solution)/shard_map/ppermute | solution.py:15
  98.3 5.8 %collective-permute-start.23 = (f32[4,1,1024]{2,1,0:T(1,128)S(1)}, f32[4,1,1024]{2,1,0:T(1,128)S(1)}, u32[]{:S(2)}, u32[]{:S(2)}) collective-permute-start(f32[4,1,1024]{2,1,0:T(1,128)S(1)} %get-tuple-element.49), channel_id=1, source_target_pairs={{1,0},{2,1},{3,2},{5,4},{6,5},{7,6},{9,8},{10,9},{11,10},{13,12},{... | collective-permute-start | bytes 49160 | tf_op jit(solution)/shard_map/ppermute | solution.py:18
  99.6 5.0 %collective-permute-start.22 = (f32[4,1,1024]{2,1,0:T(1,128)S(1)}, f32[4,1,1024]{2,1,0:T(1,128)S(1)}, u32[]{:S(2)}, u32[]{:S(2)}) collective-permute-start(f32[4,1,1024]{2,1,0:T(1,128)S(1)} %get-tuple-element.48), channel_id=1, source_target_pairs={{0,1},{1,2},{2,3},{4,5},{5,6},{6,7},{8,9},{9,10},{10,11},{12,13},{... | collective-permute-start | bytes 49160 | tf_op jit(solution)/shard_map/ppermute | solution.py:15
  105.0 6.4 %collective-permute-start.25 = (f32[4,1,1024]{2,1,0:T(1,128)S(1)}, f32[4,1,1024]{2,1,0:T(1,128)S(1)}, u32[]{:S(2)}, u32[]{:S(2)}) collective-permute-start(f32[4,1,1024]{2,1,0:T(1,128)S(1)} %get-tuple-element.47), channel_id=1, source_target_pairs={{1,0},{2,1},{3,2},{5,4},{6,5},{7,6},{9,8},{10,9},{11,10},{13,12},{... | collective-permute-start | bytes 49160 | tf_op jit(solution)/shard_map/ppermute | solution.py:18
  106.3 5.7 %collective-permute-start.24 = (f32[4,1,1024]{2,1,0:T(1,128)S(1)}, f32[4,1,1024]{2,1,0:T(1,128)S(1)}, u32[]{:S(2)}, u32[]{:S(2)}) collective-permute-start(f32[4,1,1024]{2,1,0:T(1,128)S(1)} %get-tuple-element.46), channel_id=1, source_target_pairs={{0,1},{1,2},{2,3},{4,5},{5,6},{6,7},{8,9},{9,10},{10,11},{12,13},{... | collective-permute-start | bytes 49160 | tf_op jit(solution)/shard_map/ppermute | solution.py:15
  112.3 6.4 %collective-permute-start.27 = (f32[4,1,1024]{2,1,0:T(1,128)S(1)}, f32[4,1,1024]{2,1,0:T(1,128)S(1)}, u32[]{:S(2)}, u32[]{:S(2)}) collective-permute-start(f32[4,1,1024]{2,1,0:T(1,128)S(1)} %get-tuple-element.45), channel_id=1, source_target_pairs={{1,0},{2,1},{3,2},{5,4},{6,5},{7,6},{9,8},{10,9},{11,10},{13,12},{... | collective-permute-start | bytes 49160 | tf_op jit(solution)/shard_map/ppermute | solution.py:18
  113.6 5.7 %collective-permute-start.26 = (f32[4,1,1024]{2,1,0:T(1,128)S(1)}, f32[4,1,1024]{2,1,0:T(1,128)S(1)}, u32[]{:S(2)}, u32[]{:S(2)}) collective-permute-start(f32[4,1,1024]{2,1,0:T(1,128)S(1)} %get-tuple-element.44), channel_id=1, source_target_pairs={{0,1},{1,2},{2,3},{4,5},{5,6},{6,7},{8,9},{9,10},{10,11},{12,13},{... | collective-permute-start | bytes 49160 | tf_op jit(solution)/shard_map/ppermute | solution.py:15
  119.6 6.4 %collective-permute-start.29 = (f32[4,1,1024]{2,1,0:T(1,128)S(1)}, f32[4,1,1024]{2,1,0:T(1,128)S(1)}, u32[]{:S(2)}, u32[]{:S(2)}) collective-permute-start(f32[4,1,1024]{2,1,0:T(1,128)S(1)} %get-tuple-element.43), channel_id=1, source_target_pairs={{1,0},{2,1},{3,2},{5,4},{6,5},{7,6},{9,8},{10,9},{11,10},{13,12},{... | collective-permute-start | bytes 49160 | tf_op jit(solution)/shard_map/ppermute | solution.py:18
  120.9 5.7 %collective-permute-start.28 = (f32[4,1,1024]{2,1,0:T(1,128)S(1)}, f32[4,1,1024]{2,1,0:T(1,128)S(1)}, u32[]{:S(2)}, u32[]{:S(2)}) collective-permute-start(f32[4,1,1024]{2,1,0:T(1,128)S(1)} %get-tuple-element.42), channel_id=1, source_target_pairs={{0,1},{1,2},{2,3},{4,5},{5,6},{6,7},{8,9},{9,10},{10,11},{12,13},{... | collective-permute-start | bytes 49160 | tf_op jit(solution)/shard_map/ppermute | solution.py:15
  127.0 6.4 %collective-permute-start.31 = (f32[4,1,1024]{2,1,0:T(1,128)S(1)}, f32[4,1,1024]{2,1,0:T(1,128)S(1)}, u32[]{:S(2)}, u32[]{:S(2)}) collective-permute-start(f32[4,1,1024]{2,1,0:T(1,128)S(1)} %get-tuple-element.41), channel_id=1, source_target_pairs={{1,0},{2,1},{3,2},{5,4},{6,5},{7,6},{9,8},{10,9},{11,10},{13,12},{... | collective-permute-start | bytes 49160 | tf_op jit(solution)/shard_map/ppermute | solution.py:18
  128.3 5.7 %collective-permute-start.30 = (f32[4,1,1024]{2,1,0:T(1,128)S(1)}, f32[4,1,1024]{2,1,0:T(1,128)S(1)}, u32[]{:S(2)}, u32[]{:S(2)}) collective-permute-start(f32[4,1,1024]{2,1,0:T(1,128)S(1)} %get-tuple-element.40), channel_id=1, source_target_pairs={{0,1},{1,2},{2,3},{4,5},{5,6},{6,7},{8,9},{9,10},{10,11},{12,13},{... | collective-permute-start | bytes 49160 | tf_op jit(solution)/shard_map/ppermute | solution.py:15
  134.3 6.4 %collective-permute-start.33 = (f32[4,1,1024]{2,1,0:T(1,128)S(1)}, f32[4,1,1024]{2,1,0:T(1,128)S(1)}, u32[]{:S(2)}, u32[]{:S(2)}) collective-permute-start(f32[4,1,1024]{2,1,0:T(1,128)S(1)} %get-tuple-element.39), channel_id=1, source_target_pairs={{1,0},{2,1},{3,2},{5,4},{6,5},{7,6},{9,8},{10,9},{11,10},{13,12},{... | collective-permute-start | bytes 49160 | tf_op jit(solution)/shard_map/ppermute | solution.py:18
  135.6 5.7 %collective-permute-start.32 = (f32[4,1,1024]{2,1,0:T(1,128)S(1)}, f32[4,1,1024]{2,1,0:T(1,128)S(1)}, u32[]{:S(2)}, u32[]{:S(2)}) collective-permute-start(f32[4,1,1024]{2,1,0:T(1,128)S(1)} %get-tuple-element.38), channel_id=1, source_target_pairs={{0,1},{1,2},{2,3},{4,5},{5,6},{6,7},{8,9},{9,10},{10,11},{12,13},{... | collective-permute-start | bytes 49160 | tf_op jit(solution)/shard_map/ppermute | solution.py:15
  141.6 6.4 %collective-permute-start.35 = (f32[4,1,1024]{2,1,0:T(1,128)S(1)}, f32[4,1,1024]{2,1,0:T(1,128)S(1)}, u32[]{:S(2)}, u32[]{:S(2)}) collective-permute-start(f32[4,1,1024]{2,1,0:T(1,128)S(1)} %get-tuple-element.37), channel_id=1, source_target_pairs={{1,0},{2,1},{3,2},{5,4},{6,5},{7,6},{9,8},{10,9},{11,10},{13,12},{... | collective-permute-start | bytes 49160 | tf_op jit(solution)/shard_map/ppermute | solution.py:18
  142.9 5.7 %collective-permute-start.34 = (f32[4,1,1024]{2,1,0:T(1,128)S(1)}, f32[4,1,1024]{2,1,0:T(1,128)S(1)}, u32[]{:S(2)}, u32[]{:S(2)}) collective-permute-start(f32[4,1,1024]{2,1,0:T(1,128)S(1)} %get-tuple-element.36), channel_id=1, source_target_pairs={{0,1},{1,2},{2,3},{4,5},{5,6},{6,7},{8,9},{9,10},{10,11},{12,13},{... | collective-permute-start | bytes 49160 | tf_op jit(solution)/shard_map/ppermute | solution.py:15
  148.1 13.0 %copy-start.3 = (f32[8,4]{0,1:T(4,128)S(1)}, f32[8,4]{0,1:T(4,128)}, u32[]{:S(2)}) copy-start(f32[8,4]{0,1:T(4,128)} %param.15) | copy-start | bytes 388
  154.7 16.6 %all-to-all-start = ((f32[8,1,8192]{2,1,0:T(1,128)}), f32[8,1,8192]{2,1,0:T(1,128)S(1)}, u32[]{:S(2)}, u32[]{:S(2)}) async-start(f32[8,1,8192]{2,1,0:T(1,128)} %fusion.112), calls=%async_computation | async-start | bytes 524288 | tf_op jit(solution)/shard_map/all_to_all | solution.py:127
  190.1 50.6 %all-to-all-start.1 = ((f32[8,1,8192]{2,1,0:T(1,128)}), f32[8,1,8192]{2,1,0:T(1,128)S(1)}, u32[]{:S(2)}, u32[]{:S(2)}) async-start(f32[8,1,8192]{2,1,0:T(1,128)} %copy.66), calls=%async_computation.1 | async-start | bytes 524288 | tf_op jit(solution)/shard_map/all_to_all | solution.py:141
